TPU v7x, 256 devices: a whole 4x4x8 slice. The times are simulated.
256 devices in a mesh: ctx: 8 (over z), vocab: 32 (over y, x, core).
Axes of the slice: x: 4, y: 4, z: 8, core: 2. Of those that a mesh axis runs over, the one named last changes fastest.
Arguments:
- hidden: bfloat16 [16, 128, 4096], P(None, 'ctx', 'vocab'), may hold values from -6 to 6
- head_weight: bfloat16 [4096, 128256], P(None, ('ctx', 'vocab')), may hold values from -0.09375 to 0.09375
- token_ids: int32 [16, 128], P(None, 'ctx'), may hold values from 0 to 128255
- response_mask: int32 [16, 128], P(None, 'ctx'), may hold values 0 or 1
- pair_order: int32 [16], replicated, may hold values from 0 to 15, each once
- frozen_logprob: float32 [16], replicated, may hold values from -40 to 40
Outputs:
- pair_loss: float32 [], replicated
- margins: float32 [8], replicated
- head_grad: bfloat16 [4096, 128256], P(None, ('ctx', 'vocab'))
- spread_grad: bfloat16 [4096, 128256], P(None, ('ctx', 'vocab'))
Inputs may be any that keep to these rules, and one draw needn't show every extreme that they name: `token_ids`: token ids lie in 0 to 128255. `response_mask`: mask entries are 0 or 1. pair_order names every sequence exactly once; entry p is the chosen sequence of pair p and entry 8 + p the rejected one.
All inputs are finite; a program needn't handle non-finite values.
Results may differ from a plain program's by a relative error of at most 0.0015.
Values may be sent and summed in bfloat16 or wider, within the bound.
A program may use at most 128 MiB of HBM per device.

v0:
```python
import jax
import jax.numpy as jnp
from jax import lax
from jax.sharding import Mesh
from jax.sharding import PartitionSpec as P

V = 128256
VOCAB = ("vocab_0", "vocab_1", "vocab_2")
CTX_VOCAB = ("ctx", "vocab_0", "vocab_1", "vocab_2")
strength = 0.1
loss_scale = 256.0


def laid_out(pieces, dim):
    pieces = jnp.moveaxis(pieces, 0, dim)
    lengths = pieces.shape
    return pieces.reshape(*lengths[:dim], lengths[dim] * lengths[dim + 1], *lengths[dim + 2 :])


def gather_packed(arrays, axis, dims):
    flat = jnp.concatenate([a.reshape(-1) for a in arrays])
    lines, at, finished = (lax.all_gather(flat, axis), 0, [])
    for a, dim in zip(arrays, dims):
        pieces = lines[:, at : at + a.size].reshape(-1, *a.shape)
        finished.append(laid_out(pieces, dim))
        at += a.size
    return tuple(finished)


def by_axis(shard, axes):
    for axis in axes:
        shard = lax.pmax(shard, axis)
    return shard


def by_axis_2(shard, axes):
    for axis in axes:
        shard = lax.psum(shard, axis)
    return shard


def contract_rows(block_rows, both_logits):
    return lax.dot_general(
        block_rows, both_logits, (((0,), (0,)), ((), ())), preferred_element_type=jnp.float32
    )


def shards(hidden, head_weight, token_ids, response_mask, pair_order, frozen_logprob):
    seq_rows = lax.all_gather(hidden, "ctx", axis=1, tiled=True)
    ids_all, mask_all = gather_packed((token_ids, response_mask), "ctx", (1, 1))
    token_rows = seq_rows.reshape(seq_rows.shape[0] * seq_rows.shape[1], seq_rows.shape[2])
    shard_width = head_weight.shape[1]
    whole_rows = lax.all_gather(token_rows, VOCAB, axis=1, tiled=True)
    logits = jnp.dot(whole_rows, head_weight, preferred_element_type=jnp.float32)
    offset = lax.axis_index(CTX_VOCAB) * shard_width
    local_ids = ids_all.reshape(-1) - offset
    columns = jnp.arange(shard_width).astype(jnp.int32)
    onehot = (columns[None, :] == local_ids[:, None]).astype(jnp.float32)
    picked_part = jnp.sum(onehot * logits, axis=1)
    peak_part = jnp.max(logits, axis=1)
    row_peak = by_axis(peak_part, CTX_VOCAB)
    exp_sums = jnp.sum(jnp.exp(logits - row_peak[:, None]), axis=1)
    sum_total, picked = (by_axis_2(exp_sums, CTX_VOCAB), by_axis_2(picked_part, CTX_VOCAB))
    log_norm = row_peak + jnp.log(sum_total)
    mask_flat = mask_all.reshape(-1).astype(jnp.float32)
    seq_count = ids_all.shape[0]
    policy = jnp.sum(((picked - log_norm) * mask_flat).reshape(seq_count, ids_all.shape[1]), axis=1)
    log_ratio = policy - frozen_logprob
    pair_count = pair_order.shape[0] // 2
    chosen = pair_order[:pair_count]
    rejected = pair_order[pair_count:]
    margins = strength * (log_ratio[chosen] - log_ratio[rejected])
    pair_loss = jnp.mean(jax.nn.softplus(-margins))
    weight = -loss_scale * strength * jax.nn.sigmoid(-margins) / pair_count
    seq_coef = jnp.zeros((seq_count,), jnp.float32).at[chosen].set(weight).at[rejected].set(-weight)
    token_coef = (seq_coef[:, None] * mask_all.astype(jnp.float32)).reshape(-1)
    probabilities = jnp.exp(logits - log_norm[:, None])
    grad_logits = (token_coef[:, None] * (onehot - probabilities)).astype(jnp.bfloat16)
    spread_logits = (V / 64.0 * token_coef[:, None] * probabilities).astype(jnp.bfloat16)
    both_logits = jnp.concatenate([grad_logits, spread_logits], axis=1)
    both_grads = contract_rows(whole_rows, both_logits)
    head_grad = both_grads[:, :shard_width].astype(jnp.bfloat16)
    spread_grad = both_grads[:, shard_width:].astype(jnp.bfloat16)
    return (pair_loss, margins, head_grad, spread_grad)


def solution(mesh):
    split = Mesh(
        mesh.devices.reshape(mesh.shape["ctx"], 4, 4, 2), ("ctx", "vocab_0", "vocab_1", "vocab_2")
    )
    placed = (P(None, "ctx", VOCAB), P(None, CTX_VOCAB), P(None, "ctx"), P(None, "ctx"), P(), P())
    return jax.shard_map(
        shards,
        mesh=split,
        in_specs=placed,
        out_specs=(P(), P(), P(None, CTX_VOCAB), P(None, CTX_VOCAB)),
        check_vma=False,
    )
```

profile of v0, /device:TPU:1, one launch (start us, length us, event | category | flops | bytes accessed | tf_op | source)
XLA Modules:
  0.0 282.0 jit_solution(17380326910799111413)
XLA Ops:
  7.2 0.0 all-gather.4.cloned.1.call-start
  7.2 26.5 %all_gather.14 = bf16[16,128,128]{2,1,0:T(8,128)(2,1)} all-gather(bf16[16,16,128]{2,1,0:T(8,128)(2,1)} %param.6), channel_id=1, replica_groups=mesh['ctx'=8,'vocab_0'=4,'vocab_1'=4,'vocab_2'=2] {'ctx'}, dimensions={1}, use_global_device_ids=true | all-gather | bytes 589824 | tf_op jit(solution)/shard_map/all_gather | solution.py:49
  33.7 0.0 all-gather.4.cloned.1.call-update
  33.7 0.8 reshape.60
  34.5 0.8 reshape.61
  35.3 16.1 %all-gather.1 = s32[8,1,512]{2,1,0:T(1,128)S(1)} all-gather(s32[1,1,512]{2,1,0:T(1,128)S(1)} %bitcast.21), channel_id=2, replica_groups=mesh['ctx'=8,'vocab_0'=4,'vocab_1'=4,'vocab_2'=2] {'ctx'}, dimensions={0}, use_global_device_ids=true | all-gather | bytes 18432 | tf_op jit(solution)/shard_map/all_gather | solution.py:22
  51.4 0.1 sub.49
  51.5 0.1 sub.51
  51.6 0.1 convert_element_type.33
  51.7 0.1 convert_element_type.35
  51.8 0.8 compare_select_fusion.1
  52.6 71.6 %all-gather.4.cloned.1.call-done = bf16[2048,4096]{1,0:T(8,128)(2,1)} async-done(((bf16[2048,128]{1,0:T(8,128)(2,1)}), bf16[2048,4096]{1,0:T(8,128)(2,1)}) %all-gather.4.cloned.1.call-update) | async-done | bytes 16777232 | tf_op jit(solution)/shard_map/all_gather | solution.py:53
  124.2 14.8 %fusion.9 = (f32[2048]{0:T(1024)S(1)}, f32[2048,501]{0,1:T(8,128)}) fusion(bf16[2048,4096]{1,0:T(8,128)(2,1)} %all-gather.4.cloned.1.call-done, bf16[4096,501]{0,1:T(8,128)(2,1)} %param.7), kind=kOutput, calls=%fused_computation.35 | convolution fusion | flops 8406409216 | bytes 24993792 | tf_op jit(solution)/shard_map/dot_general | solution.py:54
  139.0 0.0 copy-start.1
  139.0 14.1 %pmax.28 = f32[2048]{0:T(1024)S(1)} all-reduce(f32[2048]{0:T(1024)S(1)} %get-tuple-element.29), channel_id=1, replica_groups=mesh['ctx'=8,'vocab_0'=4,'vocab_1'=4,'vocab_2'=2] {'ctx'}, use_global_device_ids=true, to_apply=%region_6.0 | all-reduce | flops 2048 | bytes 16384 | tf_op jit(solution)/shard_map/pmax | solution.py:32
  153.1 8.2 %pmax.29 = f32[2048]{0:T(1024)S(1)} all-reduce(f32[2048]{0:T(1024)S(1)} %pmax.28), channel_id=1, replica_groups=mesh['ctx'=8,'vocab_0'=4,'vocab_1'=4,'vocab_2'=2] {'vocab_0'}, use_global_device_ids=true, to_apply=%region_7.0 | all-reduce | flops 2048 | bytes 16384 | tf_op jit(solution)/shard_map/pmax | solution.py:32
  161.3 7.4 %pmax.30 = f32[2048]{0:T(1024)S(1)} all-reduce(f32[2048]{0:T(1024)S(1)} %pmax.29), channel_id=1, replica_groups=mesh['ctx'=8,'vocab_0'=4,'vocab_1'=4,'vocab_2'=2] {'vocab_1'}, use_global_device_ids=true, to_apply=%region_8.0 | all-reduce | flops 2048 | bytes 16384 | tf_op jit(solution)/shard_map/pmax | solution.py:32
  168.7 10.1 %pmax.31 = f32[2048]{0:T(1024)S(1)} all-reduce(f32[2048]{0:T(1024)S(1)} %pmax.30), channel_id=1, replica_groups=mesh['ctx'=8,'vocab_0'=4,'vocab_1'=4,'vocab_2'=2] {'vocab_2'}, use_global_device_ids=true, to_apply=%region_9.0 | all-reduce | flops 2048 | bytes 16384 | tf_op jit(solution)/shard_map/pmax | solution.py:32
  178.8 3.3 %exponential_reduce_fusion = (f32[2048]{0:T(1024)S(1)}, f32[2048]{0:T(1024)S(1)}) fusion(f32[2048,501]{0,1:T(8,128)} %get-tuple-element.30, f32[2048]{0:T(1024)S(1)} %pmax.31, s32[2048]{0:T(1024)S(1)} %sub.51), kind=kLoop, calls=%fused_computation.11 | loop fusion | flops 5126144 | bytes 4136960 | tf_op jit(solution)/shard_map/reduce_sum | solution.py:62
  182.1 20.5 %all-reduce = (f32[2048]{0:T(1024)S(1)}, f32[2048]{0:T(1024)S(1)}) all-reduce(f32[2048]{0:T(1024)S(1)} %get-tuple-element.5, f32[2048]{0:T(1024)S(1)} %get-tuple-element.4), channel_id=1, replica_groups=mesh['ctx'=8,'vocab_0'=4,'vocab_1'=4,'vocab_2'=2] {'ctx'}, use_global_device_ids=true, to_apply=%region_1.0 | all-reduce | flops 4096 | bytes 32768 | tf_op jit(solution)/shard_map/psum | solution.py:38
  202.6 10.8 %all-reduce.2 = (f32[2048]{0:T(1024)S(1)}, f32[2048]{0:T(1024)S(1)}) all-reduce(f32[2048]{0:T(1024)S(1)} %get-tuple-element.6, f32[2048]{0:T(1024)S(1)} %get-tuple-element.7), channel_id=1, replica_groups=mesh['ctx'=8,'vocab_0'=4,'vocab_1'=4,'vocab_2'=2] {'vocab_0'}, use_global_device_ids=true, to_apply=%region_2.0 | all-reduce | flops 4096 | bytes 32768 | tf_op jit(solution)/shard_map/psum | solution.py:38
  213.4 10.9 %all-reduce.1 = (f32[2048]{0:T(1024)S(1)}, f32[2048]{0:T(1024)S(1)}) all-reduce(f32[2048]{0:T(1024)S(1)} %get-tuple-element.10, f32[2048]{0:T(1024)S(1)} %get-tuple-element.11), channel_id=1, replica_groups=mesh['ctx'=8,'vocab_0'=4,'vocab_1'=4,'vocab_2'=2] {'vocab_1'}, use_global_device_ids=true, to_apply=%region_3.0 | all-reduce | flops 4096 | bytes 32768 | tf_op jit(solution)/shard_map/psum | solution.py:38
  224.3 17.9 %all-reduce.3 = (f32[2048]{0:T(1024)S(1)}, f32[2048]{0:T(1024)S(1)}) all-reduce(f32[2048]{0:T(1024)S(1)} %get-tuple-element.8, f32[2048]{0:T(1024)S(1)} %get-tuple-element.9), channel_id=1, replica_groups=mesh['ctx'=8,'vocab_0'=4,'vocab_1'=4,'vocab_2'=2] {'vocab_2'}, use_global_device_ids=true, to_apply=%region_4.0 | all-reduce | flops 4096 | bytes 32768 | tf_op jit(solution)/shard_map/psum | solution.py:38
  242.2 0.1 bitcast_reduce_fusion
  242.3 0.0 copy-done.1
  242.3 0.6 gather_fusion.1
  243.0 0.6 gather_fusion
  243.6 0.0 copy-start
  243.7 0.6 scatter_custom_fusion
  244.3 0.8 scatter_fusion
  245.1 0.1 broadcast_multiply_fusion
  245.1 3.5 %multiply_convert_fusion.1 = (bf16[2048,501]{0,1:T(8,128)(2,1)S(1)}, bf16[2048,501]{0,1:T(8,128)(2,1)S(1)}) fusion(f32[2048,501]{0,1:T(8,128)} %get-tuple-element.30, f32[2048]{0:T(1024)S(1)} %get-tuple-element.20, f32[2048]{0:T(1024)S(1)} %get-tuple-element.15, s32[2048]{0:T(1024)S(1)} %sub.51, f32[2048]{0:T(1024)S(1)} %get-tuple-element.14), kind=kLoop, calls=%fused_computation.9 | loop fusion | flops 8208384 | bytes 8241152 | tf_op jit(solution)/shard_map/convert_element_type | solution.py:78
  248.7 20.1 %convert_bitcast_fusion = bf16[4096,1002]{0,1:T(8,128)(2,1)S(1)} fusion(bf16[2048,4096]{1,0:T(8,128)(2,1)} %all-gather.4.cloned.1.call-done, bf16[2048,501]{0,1:T(8,128)(2,1)S(1)} %get-tuple-element.24, bf16[2048,501]{0,1:T(8,128)(2,1)S(1)} %get-tuple-element.23), kind=kOutput, calls=%fused_computation.4 | convolution fusion | flops 16823083008 | bytes 29089792 | tf_op jit(solution)/shard_map/dot_general | solution.py:43
  268.7 4.0 %fusion.8 = (bf16[4096,501]{0,1:T(8,128)(2,1)}, bf16[4096,501]{0,1:T(8,128)(2,1)}) fusion(bf16[4096,1002]{0,1:T(8,128)(2,1)S(1)} %convert_bitcast_fusion), kind=kLoop, calls=%fused_computation.34 | loop fusion | bytes 16416768 | tf_op jit(solution)/shard_map/slice | solution.py:83
  272.7 0.0 copy-done
  272.7 0.6 fusion.3
  (8 shorter events, 0.1 us)
Async XLA Ops:
  7.2 117.1 %all-gather.4.cloned.1.call-start = ((), (), s32[]{:S(2)}) async-start(), calls=%async_computation | async-start | bytes 17301504 | tf_op jit(solution)/shard_map/all_gather | solution.py:53
  139.0 103.3 %copy-start.1 = (f32[16]{0:T(128)S(1)}, f32[16]{0:T(128)}, u32[]{:S(2)}) copy-start(f32[16]{0:T(128)} %param.11) | copy-start | bytes 196
  243.6 29.1 %copy-start = (f32[8]{0:T(128)}, f32[8]{0:T(128)S(1)}, u32[]{:S(2)}) copy-start(f32[8]{0:T(128)S(1)} %get-tuple-element.18) | copy-start | bytes 100
Sparse Core Ops, SparseCore 0:
  33.8 90.3 all-gather.3
where the time goes:
time: 282 us
  blocking collectives  142 us (50%)
  waiting for transfers between devices  71.7 us (25%)
  matrix products  34.9 us (12%)
  between operations  15.9 us (6%)
  local copies, waits for them, and re-layouts  8.61 us (3%)
  other arithmetic  8.44 us (3%)
    all_gather x1, waiting for transfers between devices, shards(): whole_rows = lax.all_gather(token_rows, VOCAB, axis=1, tiled=True)  71.6 us
    psum x4, blocking collectives, by_axis_2(): shard = lax.psum(shard, axis)  60.1 us
    pmax x4, blocking collectives, by_axis(): shard = lax.pmax(shard, axis)  39.7 us
    all_gather x1, blocking collectives, shards(): seq_rows = lax.all_gather(hidden, 'ctx', axis=1, tiled=True)  26.5 us
    dot_general x1, matrix products, contract_rows(): lax.dot_general(block_rows, both_logits, (((0,), (0,)), ((), ())), prefer...  20.1 us
    all_gather x1, blocking collectives, gather_packed(): lines, at, finished = (lax.all_gather(flat, axis), 0, [])  16.1 us
    dot_general x1, matrix products, shards(): jnp.dot(whole_rows, head_weight, preferred_element_type=jnp.float32)  14.8 us
  transfers between devices with their start and end apart: 1, of which 1 were waited for; matrix products, arithmetic and copies ran while one was open for 1% of the time, Pallas kernels for 0%

commit v1 on v0

--- a/solution.py
+++ b/solution.py
@@ -46,7 +46,11 @@
 
 
 def shards(hidden, head_weight, token_ids, response_mask, pair_order, frozen_logprob):
-    seq_rows = lax.all_gather(hidden, "ctx", axis=1, tiled=True)
+    size = lax.axis_size("ctx")
+    repeats = [size if d == 1 else 1 for d in range(hidden.ndim)]
+    seq_rows = lax.all_to_all(
+        jnp.tile(hidden, repeats), "ctx", split_axis=1, concat_axis=1, tiled=True
+    )
     ids_all, mask_all = gather_packed((token_ids, response_mask), "ctx", (1, 1))
     token_rows = seq_rows.reshape(seq_rows.shape[0] * seq_rows.shape[1], seq_rows.shape[2])
     shard_width = head_weight.shape[1]

time: 282 us -> 276 us (0.979)
  waiting for transfers between devices: 71.7 us -> 64.8 us
    all_gather x1 -> x0, blocking collectives: 26.5 us -> none  [shards(): seq_rows = lax.all_gather(hidden, 'ctx', axis=1, tiled=True)]
    all_to_all x0 -> x1, blocking collectives: none -> 24.9 us  [shards(): lax.all_to_all(jnp.tile(hidden, repeats), 'ctx', split_axis=1, concat_axi...]
    all_gather x1, waiting for transfers between devices: 71.6 us -> 64.8 us  [shards(): whole_rows = lax.all_gather(token_rows, VOCAB, axis=1, tiled=True)]
where the time goes in v1:
time: 276 us; the launch traced here: 275 us
  blocking collectives  141 us (51%)
  waiting for transfers between devices  64.8 us (23%)
  matrix products  34.9 us (13%)
  between operations  15.9 us (6%)
  local copies, waits for them, and re-layouts  10.5 us (4%)
  other arithmetic  8.44 us (3%)
    all_gather x1, waiting for transfers between devices, shards(): whole_rows = lax.all_gather(token_rows, VOCAB, axis=1, tiled=True)  64.8 us
    psum x4, blocking collectives, by_axis_2(): shard = lax.psum(shard, axis)  60.1 us
    pmax x4, blocking collectives, by_axis(): shard = lax.pmax(shard, axis)  39.7 us
    all_to_all x1, blocking collectives, shards(): lax.all_to_all(jnp.tile(hidden, repeats), 'ctx', split_axis=1, concat_axi...  24.9 us
    dot_general x1, matrix products, contract_rows(): lax.dot_general(block_rows, both_logits, (((0,), (0,)), ((), ())), prefer...  20.1 us
    all_gather x1, blocking collectives, gather_packed(): lines, at, finished = (lax.all_gather(flat, axis), 0, [])  16 us
    dot_general x1, matrix products, shards(): jnp.dot(whole_rows, head_weight, preferred_element_type=jnp.float32)  14.8 us
  transfers between devices with their start and end apart: 1, of which 1 were waited for; matrix products, arithmetic and copies ran while one was open for 1% of the time, Pallas kernels for 0%

profile of v1, /device:TPU:1, one launch (start us, length us, event | category | flops | bytes accessed | tf_op | source)
XLA Modules:
  0.0 275.3 jit_solution(18436046246247393218)
XLA Ops:
  7.2 0.0 all-gather.4.cloned.1.call-start
  7.2 0.9 copy.20
  8.1 0.1 tile.4
  8.1 24.9 %all_to_all.5 = bf16[16,128,128]{2,0,1:T(8,128)(2,1)S(1)} all-to-all(bf16[16,128,128]{2,0,1:T(8,128)(2,1)S(1)} %bitcast.19), channel_id=1, replica_groups=mesh['ctx'=8,'vocab_0'=4,'vocab_1'=4,'vocab_2'=2] {'ctx'}, dimensions={1} | all-to-all | bytes 1048576 | tf_op jit(solution)/shard_map/all_to_all | solution.py:51
  33.1 0.9 copy.21
  34.0 0.0 all-gather.4.cloned.1.call-update
  34.0 0.8 reshape.64
  34.8 0.8 reshape.65
  35.6 16.0 %all-gather.1 = s32[8,1,512]{2,1,0:T(1,128)S(1)} all-gather(s32[1,1,512]{2,1,0:T(1,128)S(1)} %bitcast.23), channel_id=2, replica_groups=mesh['ctx'=8,'vocab_0'=4,'vocab_1'=4,'vocab_2'=2] {'ctx'}, dimensions={0}, use_global_device_ids=true | all-gather | bytes 18432 | tf_op jit(solution)/shard_map/all_gather | solution.py:22
  51.6 0.1 sub.49
  51.7 0.1 sub.51
  51.8 0.1 convert_element_type.33
  51.9 0.1 convert_element_type.35
  52.0 0.8 compare_select_fusion.1
  52.8 64.8 %all-gather.4.cloned.1.call-done = bf16[2048,4096]{1,0:T(8,128)(2,1)} async-done(((bf16[2048,128]{1,0:T(8,128)(2,1)}), bf16[2048,4096]{1,0:T(8,128)(2,1)}) %all-gather.4.cloned.1.call-update) | async-done | bytes 16777232 | tf_op jit(solution)/shard_map/all_gather | solution.py:57
  117.6 14.8 %fusion.9 = (f32[2048]{0:T(1024)S(1)}, f32[2048,501]{0,1:T(8,128)}) fusion(bf16[2048,4096]{1,0:T(8,128)(2,1)} %all-gather.4.cloned.1.call-done, bf16[4096,501]{0,1:T(8,128)(2,1)} %param.7), kind=kOutput, calls=%fused_computation.35 | convolution fusion | flops 8406409216 | bytes 24993792 | tf_op jit(solution)/shard_map/dot_general | solution.py:58
  132.4 0.0 copy-start.1
  132.4 14.1 %pmax.28 = f32[2048]{0:T(1024)S(1)} all-reduce(f32[2048]{0:T(1024)S(1)} %get-tuple-element.29), channel_id=1, replica_groups=mesh['ctx'=8,'vocab_0'=4,'vocab_1'=4,'vocab_2'=2] {'ctx'}, use_global_device_ids=true, to_apply=%region_6.0 | all-reduce | flops 2048 | bytes 16384 | tf_op jit(solution)/shard_map/pmax | solution.py:32
  146.5 8.2 %pmax.29 = f32[2048]{0:T(1024)S(1)} all-reduce(f32[2048]{0:T(1024)S(1)} %pmax.28), channel_id=1, replica_groups=mesh['ctx'=8,'vocab_0'=4,'vocab_1'=4,'vocab_2'=2] {'vocab_0'}, use_global_device_ids=true, to_apply=%region_7.0 | all-reduce | flops 2048 | bytes 16384 | tf_op jit(solution)/shard_map/pmax | solution.py:32
  154.7 7.4 %pmax.30 = f32[2048]{0:T(1024)S(1)} all-reduce(f32[2048]{0:T(1024)S(1)} %pmax.29), channel_id=1, replica_groups=mesh['ctx'=8,'vocab_0'=4,'vocab_1'=4,'vocab_2'=2] {'vocab_1'}, use_global_device_ids=true, to_apply=%region_8.0 | all-reduce | flops 2048 | bytes 16384 | tf_op jit(solution)/shard_map/pmax | solution.py:32
  162.1 10.1 %pmax.31 = f32[2048]{0:T(1024)S(1)} all-reduce(f32[2048]{0:T(1024)S(1)} %pmax.30), channel_id=1, replica_groups=mesh['ctx'=8,'vocab_0'=4,'vocab_1'=4,'vocab_2'=2] {'vocab_2'}, use_global_device_ids=true, to_apply=%region_9.0 | all-reduce | flops 2048 | bytes 16384 | tf_op jit(solution)/shard_map/pmax | solution.py:32
  172.2 3.3 %exponential_reduce_fusion = (f32[2048]{0:T(1024)S(1)}, f32[2048]{0:T(1024)S(1)}) fusion(f32[2048,501]{0,1:T(8,128)} %get-tuple-element.30, f32[2048]{0:T(1024)S(1)} %pmax.31, s32[2048]{0:T(1024)S(1)} %sub.51), kind=kLoop, calls=%fused_computation.11 | loop fusion | flops 5126144 | bytes 4136960 | tf_op jit(solution)/shard_map/reduce_sum | solution.py:66
  175.4 20.5 %all-reduce = (f32[2048]{0:T(1024)S(1)}, f32[2048]{0:T(1024)S(1)}) all-reduce(f32[2048]{0:T(1024)S(1)} %get-tuple-element.5, f32[2048]{0:T(1024)S(1)} %get-tuple-element.4), channel_id=1, replica_groups=mesh['ctx'=8,'vocab_0'=4,'vocab_1'=4,'vocab_2'=2] {'ctx'}, use_global_device_ids=true, to_apply=%region_1.0 | all-reduce | flops 4096 | bytes 32768 | tf_op jit(solution)/shard_map/psum | solution.py:38
  196.0 10.8 %all-reduce.2 = (f32[2048]{0:T(1024)S(1)}, f32[2048]{0:T(1024)S(1)}) all-reduce(f32[2048]{0:T(1024)S(1)} %get-tuple-element.6, f32[2048]{0:T(1024)S(1)} %get-tuple-element.7), channel_id=1, replica_groups=mesh['ctx'=8,'vocab_0'=4,'vocab_1'=4,'vocab_2'=2] {'vocab_0'}, use_global_device_ids=true, to_apply=%region_2.0 | all-reduce | flops 4096 | bytes 32768 | tf_op jit(solution)/shard_map/psum | solution.py:38
  206.8 10.8 %all-reduce.1 = (f32[2048]{0:T(1024)S(1)}, f32[2048]{0:T(1024)S(1)}) all-reduce(f32[2048]{0:T(1024)S(1)} %get-tuple-element.10, f32[2048]{0:T(1024)S(1)} %get-tuple-element.11), channel_id=1, replica_groups=mesh['ctx'=8,'vocab_0'=4,'vocab_1'=4,'vocab_2'=2] {'vocab_1'}, use_global_device_ids=true, to_apply=%region_3.0 | all-reduce | flops 4096 | bytes 32768 | tf_op jit(solution)/shard_map/psum | solution.py:38
  217.6 17.9 %all-reduce.3 = (f32[2048]{0:T(1024)S(1)}, f32[2048]{0:T(1024)S(1)}) all-reduce(f32[2048]{0:T(1024)S(1)} %get-tuple-element.8, f32[2048]{0:T(1024)S(1)} %get-tuple-element.9), channel_id=1, replica_groups=mesh['ctx'=8,'vocab_0'=4,'vocab_1'=4,'vocab_2'=2] {'vocab_2'}, use_global_device_ids=true, to_apply=%region_4.0 | all-reduce | flops 4096 | bytes 32768 | tf_op jit(solution)/shard_map/psum | solution.py:38
  235.5 0.1 bitcast_reduce_fusion
  235.7 0.0 copy-done.1
  235.7 0.6 gather_fusion.1
  236.3 0.6 gather_fusion
  237.0 0.0 copy-start
  237.0 0.6 scatter_custom_fusion
  237.6 0.8 scatter_fusion
  238.4 0.1 broadcast_multiply_fusion
  238.5 3.5 %multiply_convert_fusion.1 = (bf16[2048,501]{0,1:T(8,128)(2,1)S(1)}, bf16[2048,501]{0,1:T(8,128)(2,1)S(1)}) fusion(f32[2048,501]{0,1:T(8,128)} %get-tuple-element.30, f32[2048]{0:T(1024)S(1)} %get-tuple-element.20, f32[2048]{0:T(1024)S(1)} %get-tuple-element.15, s32[2048]{0:T(1024)S(1)} %sub.51, f32[2048]{0:T(1024)S(1)} %get-tuple-element.14), kind=kLoop, calls=%fused_computation.9 | loop fusion | flops 8208384 | bytes 8241152 | tf_op jit(solution)/shard_map/convert_element_type | solution.py:82
  242.0 20.1 %convert_bitcast_fusion = bf16[4096,1002]{0,1:T(8,128)(2,1)S(1)} fusion(bf16[2048,4096]{1,0:T(8,128)(2,1)} %all-gather.4.cloned.1.call-done, bf16[2048,501]{0,1:T(8,128)(2,1)S(1)} %get-tuple-element.24, bf16[2048,501]{0,1:T(8,128)(2,1)S(1)} %get-tuple-element.23), kind=kOutput, calls=%fused_computation.4 | convolution fusion | flops 16823083008 | bytes 29089792 | tf_op jit(solution)/shard_map/dot_general | solution.py:43
  262.1 4.0 %fusion.8 = (bf16[4096,501]{0,1:T(8,128)(2,1)}, bf16[4096,501]{0,1:T(8,128)(2,1)}) fusion(bf16[4096,1002]{0,1:T(8,128)(2,1)S(1)} %convert_bitcast_fusion), kind=kLoop, calls=%fused_computation.34 | loop fusion | bytes 16416768 | tf_op jit(solution)/shard_map/slice | solution.py:87
  266.1 0.0 copy-done
  266.1 0.6 fusion.3
  (8 shorter events, 0.1 us)
Async XLA Ops:
  7.2 110.4 %all-gather.4.cloned.1.call-start = ((), (), s32[]{:S(2)}) async-start(), calls=%async_computation.1 | async-start | bytes 17301504 | tf_op jit(solution)/shard_map/all_gather | solution.py:57
  132.4 103.3 %copy-start.1 = (f32[16]{0:T(128)S(1)}, f32[16]{0:T(128)}, u32[]{:S(2)}) copy-start(f32[16]{0:T(128)} %param.11) | copy-start | bytes 196
  237.0 29.1 %copy-start = (f32[8]{0:T(128)}, f32[8]{0:T(128)S(1)}, u32[]{:S(2)}) copy-start(f32[8]{0:T(128)S(1)} %get-tuple-element.18) | copy-start | bytes 100
Sparse Core Ops, SparseCore 0:
  34.1 83.3 all-gather.3
